TPU v7x, 256 devices: a whole 4x4x8 slice. The times are simulated.
256 devices in a mesh: dp: 32 (over z, y_lo, core), expert: 8 (over y_hi, x).
Axes of the slice: x: 4, y: 4 (y_hi: 2, y_lo: 2; y = y_hi * 2 + y_lo), z: 8, core: 2. Of those that a mesh axis runs over, the one named last changes fastest.
Arguments:
- tokens: bfloat16 [2048, 6144], P(('dp', 'expert')), may hold values from -6 to 6
- router_now: float32 [6144, 8], P('dp'), may hold values from -0.078125 to 0.078125
- router_next: float32 [6144, 8], P('dp'), may hold values from -0.078125 to 0.078125
- w_gate: bfloat16 [8, 6144, 8192], P('expert', None, 'dp'), may hold values from -0.078125 to 0.078125
- w_up: bfloat16 [8, 6144, 8192], P('expert', None, 'dp'), may hold values from -0.078125 to 0.078125
- w_down: bfloat16 [8, 8192, 6144], P('expert', 'dp'), may hold values from -0.0625 to 0.0625
- expert_ids: int32 [2048, 2], P(('dp', 'expert')), may hold values from 0 to 7, all different within a row; in each aligned block of 8 rows (0 to 7, 8 to 15, ...) at most 4 rows name the same one
- next_ids: int32 [2048, 2], P(('dp', 'expert')), may hold values from 0 to 7, all different within a row
Outputs:
- layer_out: bfloat16 [2048, 6144], P(('dp', 'expert'))
- next_logits: float32 [2048, 8], P(('dp', 'expert'))
- next_weights: float32 [2048, 2], P(('dp', 'expert'))
Inputs may be any that keep to these rules, and one draw needn't show every extreme that they name: `expert_ids`: each row names 2 different experts. Among the 8 rows of one device no expert is named by more than 4 rows, and on some devices one expert is named by exactly 4 rows. `next_ids`: each row names 2 different experts.
All inputs are finite; a program needn't handle non-finite values.
Results may differ from a plain program's by a relative error of at most 0.013.
Values may be sent and summed in bfloat16 or wider, within the bound.
No kernel may reach another device: no remote copies, remote signals or barrier semaphores. Data moves between devices by JAX's collectives and lax.ppermute only.
A program may use at most 128 MiB of HBM per device.

v0:
```python
import jax
import jax.numpy as jnp
from jax import lax
from jax.sharding import PartitionSpec as P

CAP = 4
epsilon = 1e-05


def in_one_piece(arrays, axis, dim, along):
    both = jnp.concatenate(arrays, axis=along)
    filled, at, outs = (lax.all_gather(both, axis, axis=dim, tiled=True), 0, [])
    for a in arrays:
        outs.append(lax.slice_in_dim(filled, at, at + a.shape[along], axis=along))
        at += a.shape[along]
    return tuple(outs)


def rms_normed(values):
    return values * lax.rsqrt(jnp.mean(values * values, axis=-1, keepdims=True) + epsilon)


def pair_weights(logits, chosen):
    picked = jnp.take_along_axis(logits, chosen, axis=1)
    first = jax.nn.sigmoid(picked[:, 0] - picked[:, 1])
    return jnp.stack([first, 1.0 - first], axis=1)


def on_device(tokens, router_now, router_next, w_gate, w_up, w_down, expert_ids, next_ids):
    whole_now, whole_next = in_one_piece((router_now, router_next), "dp", 0, 1)
    resid = tokens.astype(jnp.float32)
    normed = rms_normed(resid)
    logits = jnp.dot(
        normed, whole_now, precision=lax.Precision.HIGHEST, preferred_element_type=jnp.float32
    )
    weights = pair_weights(logits, expert_ids)
    rounded = normed.astype(jnp.bfloat16)
    expert_count = whole_now.shape[1]
    per_device = w_gate.shape[0]
    groups = lax.axis_size("expert")
    tok_count = tokens.shape[0]
    top_count = expert_ids.shape[1]
    width = tokens.shape[1]
    pairs = tok_count * top_count
    chosen = expert_ids.reshape(pairs)
    onehot = (chosen[:, None] == jnp.arange(expert_count, dtype=jnp.int32)[None, :]).astype(
        jnp.int32
    )
    ranks = jnp.sum((jnp.cumsum(onehot, axis=0) - onehot) * onehot, axis=1)
    places = chosen * CAP + ranks
    place_table = (
        places[:, None] == jnp.arange(expert_count * CAP, dtype=jnp.int32)[None, :]
    ).astype(jnp.float32)
    owners = (
        (jnp.arange(pairs, dtype=jnp.int32) // top_count)[:, None]
        == jnp.arange(tok_count, dtype=jnp.int32)[None, :]
    ).astype(jnp.float32)
    sender = jnp.dot(place_table.T, owners, preferred_element_type=jnp.float32)
    dispatched = jnp.dot(
        sender.astype(jnp.bfloat16), rounded, preferred_element_type=jnp.float32
    ).astype(jnp.bfloat16)
    dispatched = dispatched.reshape(groups, per_device, CAP, width)
    received = lax.all_to_all(dispatched, "expert", split_axis=0, concat_axis=0, tiled=True)
    combine = jnp.sum(
        (place_table * weights.reshape(pairs)[:, None]).reshape(
            tok_count, top_count, expert_count * CAP
        ),
        axis=1,
    )
    hidden_list = []
    local = 0
    arriving = received[:, local].reshape(groups * CAP, width)

    def activate(piece, start, local=local):
        gate = jnp.dot(piece, w_gate[local], preferred_element_type=jnp.float32)
        upward = jnp.dot(piece, w_up[local], preferred_element_type=jnp.float32)
        return (jax.nn.silu(gate) * upward).astype(jnp.bfloat16)

    hidden_list.append(activate(lax.all_gather(arriving, "dp", axis=0, tiled=True), jnp.int32(0)))
    local = 0

    def project(start, count, local=local):
        block = hidden_list[local]
        return jnp.dot(block, w_down[local], preferred_element_type=jnp.float32)

    reduced = lax.psum_scatter(
        project(jnp.int32(0), groups * CAP * lax.axis_size("dp")).astype(jnp.bfloat16),
        "dp",
        scatter_dimension=0,
        tiled=True,
    ).astype(jnp.float32)
    returned_rows = [reduced.reshape(groups, CAP, width)]
    stacked = jnp.stack(returned_rows, axis=1)
    back = (
        lax.all_to_all(
            stacked.astype(jnp.bfloat16), "expert", split_axis=0, concat_axis=0, tiled=True
        )
        .astype(stacked.dtype)
        .reshape(expert_count * CAP, width)
    )
    mixture = jnp.dot(
        combine, back, precision=lax.Precision.HIGHEST, preferred_element_type=jnp.float32
    )
    summed = resid + mixture
    layer_out = summed.astype(jnp.bfloat16)
    next_logits = jnp.dot(
        rms_normed(summed),
        whole_next,
        precision=lax.Precision.HIGHEST,
        preferred_element_type=jnp.float32,
    )
    next_weights = pair_weights(next_logits, next_ids)
    return (layer_out, next_logits, next_weights)


def solution(mesh):
    in_specs = (
        P(("dp", "expert"), None),
        P("dp", None),
        P("dp", None),
        P("expert", None, "dp"),
        P("expert", None, "dp"),
        P("expert", "dp", None),
        P(("dp", "expert"), None),
        P(("dp", "expert"), None),
    )
    out_specs = (P(("dp", "expert"), None), P(("dp", "expert"), None), P(("dp", "expert"), None))
    return jax.shard_map(
        on_device, mesh=mesh, in_specs=in_specs, out_specs=out_specs, check_vma=False
    )
```

profile of v0, /device:TPU:2, one launch (start us, length us, event | category | flops | bytes accessed | tf_op | source)
XLA Modules:
  0.0 328.4 jit_solution(14889637307065772511)
XLA Ops:
  7.2 0.9 copy.58
  8.3 0.2 select_reduce_fusion.1
  8.5 0.5 and_select_fusion.2
  9.0 1.1 fusion.21
  10.1 1.5 convolution_convert_fusion.1
  11.6 0.9 reshape.88
  12.4 16.5 %all_to_all.10 = bf16[8,1,4,6144]{3,2,1,0:T(4,128)(2,1)S(1)} all-to-all(bf16[8,1,4,6144]{3,2,1,0:T(4,128)(2,1)} %bitcast.34), channel_id=1, replica_groups=mesh['dp'=32,'expert'=8] {'expert'}, dimensions={0} | all-to-all | bytes 786432 | tf_op jit(solution)/shard_map/all_to_all | solution.py:63
  28.9 0.8 reshape_squeeze.3
  29.8 79.3 %all-gather.3.cloned.1.call-done = bf16[1024,6144]{1,0:T(8,128)(2,1)} async-done(((bf16[32,6144]{1,0:T(8,128)(2,1)}), bf16[1024,6144]{1,0:T(8,128)(2,1)}) %all-gather.3.cloned.1.call-update) | async-done | bytes 12582928 | tf_op jit(solution)/shard_map/all_gather | solution.py:79
  109.1 9.9 %fusion.3 = f32[1024,256]{1,0:T(8,128)} fusion(bf16[1024,6144]{1,0:T(8,128)(2,1)} %all-gather.3.cloned.1.call-done, bf16[1,6144,256]{2,1,0:T(8,128)(2,1)} %param.13), kind=kOutput, calls=%fused_computation.8 | convolution fusion | flops 3221225472 | bytes 16777216 | tf_op jit(solution)/shard_map/dot_general | solution.py:75
  119.0 19.8 %convolution_convert_fusion = bf16[1024,6144]{1,0:T(8,128)(2,1)} fusion(bf16[1,256,6144]{2,1,0:T(8,128)(2,1)S(1)} %copy-done, bf16[1024,6144]{1,0:T(8,128)(2,1)} %all-gather.3.cloned.1.call-done, bf16[1,6144,256]{2,1,0:T(8,128)(2,1)} %param.14, f32[1024,256]{1,0:T(8,128)} %fusion.3), kind=kOutput, calls=%fused_computation.2 | convolution fusion | flops 6450315264 | bytes 32505856 | tf_op jit(solution)/shard_map/dot_general | solution.py:84
  139.0 0.6 multiply_add_fusion
  139.7 0.1 copy.66
  139.9 36.9 %all-gather = f32[32,192,16]{1,2,0:T(8,128)S(1)} all-gather(f32[1,192,16]{1,2,0:T(8,128)S(1)} %maximum_bitcast_fusion), channel_id=1, replica_groups=mesh['dp'=32,'expert'=8] {'dp'}, dimensions={0}, use_global_device_ids=true | all-gather | bytes 405504 | tf_op jit(solution)/shard_map/all_gather | solution.py:12
  176.8 1.1 copy.64
  177.9 1.3 reshape.114
  179.1 1.5 fusion.20
  180.6 0.7 gather_fusion
  181.4 0.8 copy.70
  182.1 0.6 clamp_shift-left_fusion
  182.8 106.2 %reduce-scatter.2.cloned.1.call-done = bf16[32,6144]{1,0:T(8,128)(2,1)} async-done(((bf16[1024,6144]{1,0:T(8,128)(2,1)}), bf16[32,6144]{1,0:T(8,128)(2,1)}) %reduce-scatter.2.cloned.1.call-update) | async-done | bytes 393232 | tf_op jit(solution)/shard_map/reduce_scatter | solution.py:86
  289.1 1.9 convert_element_type.47
  290.9 16.1 %all-to-all-start.1 = ((bf16[8,1,4,6144]{3,2,1,0:T(4,128)(2,1)}), bf16[8,1,4,6144]{3,2,1,0:T(4,128)(2,1)}, u32[]{:S(2)}, u32[]{:S(2)}) async-start(bf16[8,1,4,6144]{3,2,1,0:T(4,128)(2,1)} %bitcast.33), calls=%async_computation.2 | async-start | bytes 786432 | tf_op jit(solution)/shard_map/all_to_all | solution.py:95
  307.2 1.3 copy.60
  308.6 0.8 copy.73
  309.5 0.8 select_reduce_fusion
  310.3 5.2 %all-to-all-done.1 = bf16[8,1,4,6144]{3,2,1,0:T(4,128)(2,1)} async-done(((bf16[8,1,4,6144]{3,2,1,0:T(4,128)(2,1)}), bf16[8,1,4,6144]{3,2,1,0:T(4,128)(2,1)}, u32[]{:S(2)}, u32[]{:S(2)}) %all-to-all-start.1) | async-done | bytes 393248 | tf_op jit(solution)/shard_map/all_to_all | solution.py:95
  315.5 1.8 reshape.89
  317.3 2.0 multiply_reduce_fusion
  319.4 0.6 fusion.22
  320.0 0.7 gather_fusion.1
  321.0 0.6 pad_maximum_fusion.1
  (35 shorter events, 1.4 us)
Async XLA Ops:
  7.2 111.9 %copy-start = (bf16[1,256,6144]{2,1,0:T(8,128)(2,1)S(1)}, bf16[1,256,6144]{2,1,0:T(8,128)(2,1)}, u32[]{:S(2)}) copy-start(bf16[1,256,6144]{2,1,0:T(8,128)(2,1)} %param.15) | copy-start | bytes 9437188
  7.2 101.9 %all-gather.3.cloned.1.call-start = ((), (), s32[]{:S(2)}) async-start(), calls=%async_computation.3 | async-start | bytes 12976128 | tf_op jit(solution)/shard_map/all_gather | solution.py:79
  29.8 259.3 %reduce-scatter.2.cloned.1.call-start = ((), (), s32[]{:S(2)}) async-start(), calls=%async_computation.4 | async-start | bytes 12976128 | tf_op jit(solution)/shard_map/reduce_scatter | solution.py:86
  138.9 1.0 copy-start.2
  138.9 1.0 copy-start.3
  290.9 24.6 %all-to-all-start.1 = ((bf16[8,1,4,6144]{3,2,1,0:T(4,128)(2,1)}), bf16[8,1,4,6144]{3,2,1,0:T(4,128)(2,1)}, u32[]{:S(2)}, u32[]{:S(2)}) async-start(bf16[8,1,4,6144]{3,2,1,0:T(4,128)(2,1)} %bitcast.33), calls=%async_computation.2 | async-start | bytes 786432 | tf_op jit(solution)/shard_map/all_to_all | solution.py:95
  320.0 1.6 copy-start.1
Sparse Core Ops, SparseCore 0:
  29.9 79.1 all-gather.2
  139.0 149.9 reduce-scatter.1
where the time goes:
time: 329 us; the launch traced here: 328 us
  waiting for transfers between devices  191 us (58%)
  blocking collectives  53.4 us (16%)
  matrix products  35.4 us (11%)
  starting transfers between devices  16.2 us (5%)
  between operations  14.1 us (4%)
  local copies, waits for them, and re-layouts  13.9 us (4%)
  other arithmetic  4.72 us (1%)
    reduce_scatter x1, waiting for transfers between devices, on_device(): lax.psum_scatter(project(jnp.int32(0), groups * CAP * lax.axis_size('dp')...  106 us
    all_gather x1, waiting for transfers between devices, on_device(): lax.all_gather(arriving, 'dp', axis=0, tiled=True)  79.3 us
    all_gather x1, blocking collectives, in_one_piece(): filled, at, outs = (lax.all_gather(both, axis, axis=dim, tiled=True), 0, [])  36.9 us
    dot_general x1, matrix products, project(): return jnp.dot(block, w_down[local], preferred_element_type=jnp.float32)  19.8 us
    all_to_all x1, blocking collectives, on_device(): lax.all_to_all(dispatched, 'expert', split_axis=0, concat_axis=0, tiled=T...  16.5 us
    all_to_all x1, starting transfers between devices, on_device(): lax.all_to_all(stacked.astype(jnp.bfloat16), 'expert', split_axis=0, conc...  16.1 us
    dot_general x1, matrix products, activate(): gate = jnp.dot(piece, w_gate[local], preferred_element_type=jnp.float32)  9.95 us
  transfers between devices with their start and end apart: 3, of which 3 were waited for; matrix products, arithmetic and copies ran while one was open for 3% of the time, Pallas kernels for 0%

commit v1 on v0

--- a/solution.py
+++ b/solution.py
@@ -5,6 +5,13 @@
 
 CAP = 4
 epsilon = 1e-05
+
+
+def exchange_gather(x, name, along):
+    size = lax.axis_size(name)
+    tiles = jnp.stack([x for _ in range(size)])
+    tiles = lax.all_to_all(tiles, name, split_axis=0, concat_axis=0)
+    return jnp.concatenate(tiles, axis=along)
 
 
 def in_one_piece(arrays, axis, dim, along):
@@ -76,7 +83,7 @@
         upward = jnp.dot(piece, w_up[local], preferred_element_type=jnp.float32)
         return (jax.nn.silu(gate) * upward).astype(jnp.bfloat16)
 
-    hidden_list.append(activate(lax.all_gather(arriving, "dp", axis=0, tiled=True), jnp.int32(0)))
+    hidden_list.append(activate(exchange_gather(arriving, "dp", 0), jnp.int32(0)))
     local = 0
 
     def project(start, count, local=local):

time: 329 us -> 531 us (1.61)
  blocking collectives: 53.4 us -> 340 us
  waiting for transfers between devices: 191 us -> 106 us
  local copies, waits for them, and re-layouts: 13.9 us -> 24.8 us
  starting transfers between devices: 16.2 us -> 7.57 us
  matrix products: 35.4 us -> 29.9 us
    all_to_all x0 -> x1, blocking collectives: none -> 285 us  [exchange_gather(): tiles = lax.all_to_all(tiles, name, split_axis=0, concat_axis=0)]
    all_gather x1 -> x0, waiting for transfers between devices: 79.3 us -> none  [on_device(): lax.all_gather(arriving, 'dp', axis=0, tiled=True)]
    all_to_all x1, starting transfers between devices: 16.1 us -> 7.53 us  [on_device(): lax.all_to_all(stacked.astype(jnp.bfloat16), 'expert', split_axis=0, conc...]
    reduce_scatter x1, waiting for transfers between devices: 106 us -> 99.2 us  [on_device(): lax.psum_scatter(project(jnp.int32(0), groups * CAP * lax.axis_size('dp')...]
    another operation x1 -> x2, local copies, waits for them, and re-layouts: 0.83 us -> 7.22 us  [exchange_gather(): tiles = jnp.stack([x for _ in range(size)])]
    dot_general x1, matrix products: 9.95 us -> 4.48 us  [activate(): gate = jnp.dot(piece, w_gate[local], preferred_element_type=jnp.float32)]
  transfers between devices with their start and end apart: 3 -> 2, of which waited for: 3 -> 2; matrix products, arithmetic and copies ran while one was open for 3% -> 2% of each run, Pallas kernels for 0% -> 0%
where the time goes in v1:
time: 531 us; the launch traced here: 528 us
  blocking collectives  340 us (64%)
  waiting for transfers between devices  106 us (20%)
  matrix products  29.9 us (6%)
  local copies, waits for them, and re-layouts  24.8 us (5%)
  between operations  14.1 us (3%)
  starting transfers between devices  7.57 us (1%)
    all_to_all x1, blocking collectives, exchange_gather(): tiles = lax.all_to_all(tiles, name, split_axis=0, concat_axis=0)  285 us
    reduce_scatter x1, waiting for transfers between devices, on_device(): lax.psum_scatter(project(jnp.int32(0), groups * CAP * lax.axis_size('dp')...  99.2 us
    all_gather x1, blocking collectives, in_one_piece(): filled, at, outs = (lax.all_gather(both, axis, axis=dim, tiled=True), 0, [])  38.6 us
    dot_general x1, matrix products, project(): return jnp.dot(block, w_down[local], preferred_element_type=jnp.float32)  19.8 us
    all_to_all x1, blocking collectives, on_device(): lax.all_to_all(dispatched, 'expert', split_axis=0, concat_axis=0, tiled=T...  16.6 us
  transfers between devices with their start and end apart: 2, of which 2 were waited for; matrix products, arithmetic and copies ran while one was open for 2% of the time, Pallas kernels for 0%

profile of v1, /device:TPU:2, one launch (start us, length us, event | category | flops | bytes accessed | tf_op | source)
XLA Modules:
  0.0 527.5 jit_solution(17736521716468296167)
XLA Ops:
  7.2 0.9 copy.58
  8.5 0.5 and_select_fusion.2
  9.0 1.1 fusion.21
  10.1 1.5 convolution_convert_fusion.1
  11.6 0.9 reshape.93
  12.4 16.6 %all_to_all.15 = bf16[8,1,4,6144]{3,2,1,0:T(4,128)(2,1)} all-to-all(bf16[8,1,4,6144]{3,2,1,0:T(4,128)(2,1)} %bitcast.37), channel_id=1, replica_groups=mesh['dp'=32,'expert'=8] {'expert'}, dimensions={0} | all-to-all | bytes 786432 | tf_op jit(solution)/shard_map/all_to_all | solution.py:70
  29.0 1.1 stack_reshape_squeeze.2
  30.1 6.1 %stack.14 = bf16[32,32,6144]{2,1,0:T(8,128)(2,1)} broadcast(bf16[32,6144]{1,0:T(8,128)(2,1)S(1)} %stack_reshape_squeeze.2), dimensions={1,2} | broadcast | bytes 12976128 | tf_op jit(solution)/shard_map/stack | solution.py:12
  36.3 285.0 %all_to_all.16 = bf16[32,32,6144]{2,1,0:T(8,128)(2,1)S(1)} all-to-all(bf16[32,32,6144]{2,1,0:T(8,128)(2,1)} %stack.14), channel_id=1, replica_groups=mesh['dp'=32,'expert'=8] {'dp'}, dimensions={0} | all-to-all | bytes 25165824 | tf_op jit(solution)/shard_map/all_to_all | solution.py:13
  321.3 4.5 copy-done.2
  325.7 4.5 fusion.3
  330.2 19.8 %convolution_convert_fusion = bf16[1024,6144]{1,0:T(8,128)(2,1)} fusion(bf16[1,256,6144]{2,1,0:T(8,128)(2,1)S(1)} %copy-done, bf16[1024,6144]{1,0:T(8,128)(2,1)} %bitcast.35, bf16[1,6144,256]{2,1,0:T(8,128)(2,1)} %param.14, f32[1024,256]{1,0:T(8,128)} %fusion.3), kind=kOutput, calls=%fused_computation.2 | convolution fusion | flops 6450315264 | bytes 32505856 | tf_op jit(solution)/shard_map/dot_general | solution.py:91
  350.2 0.6 multiply_add_fusion
  351.0 38.6 %all-gather = f32[32,192,16]{1,2,0:T(8,128)S(1)} all-gather(f32[1,192,16]{1,2,0:T(8,128)S(1)} %maximum_bitcast_fusion), channel_id=1, replica_groups=mesh['dp'=32,'expert'=8] {'dp'}, dimensions={0}, use_global_device_ids=true | all-gather | bytes 405504 | tf_op jit(solution)/shard_map/all_gather | solution.py:19
  389.7 1.1 copy.64
  390.8 1.3 reshape.120
  392.0 1.5 fusion.20
  393.5 0.7 gather_fusion
  394.3 0.8 copy.70
  395.0 0.6 clamp_shift-left_fusion
  395.7 99.2 %reduce-scatter.2.cloned.1.call-done = bf16[32,6144]{1,0:T(8,128)(2,1)} async-done(((bf16[1024,6144]{1,0:T(8,128)(2,1)}), bf16[32,6144]{1,0:T(8,128)(2,1)}) %reduce-scatter.2.cloned.1.call-update) | async-done | bytes 393232 | tf_op jit(solution)/shard_map/reduce_scatter | solution.py:93
  494.9 1.9 convert_element_type.47
  496.8 7.5 %all-to-all-start.2 = ((bf16[8,1,4,6144]{3,2,1,0:T(4,128)(2,1)}), bf16[8,1,4,6144]{3,2,1,0:T(4,128)(2,1)}, u32[]{:S(2)}, u32[]{:S(2)}) async-start(bf16[8,1,4,6144]{3,2,1,0:T(4,128)(2,1)} %bitcast.36), calls=%async_computation.3 | async-start | bytes 786432 | tf_op jit(solution)/shard_map/all_to_all | solution.py:102
  504.5 1.3 copy.60
  505.8 0.8 copy.73
  506.7 0.8 select_reduce_fusion
  507.5 7.1 %all-to-all-done.2 = bf16[8,1,4,6144]{3,2,1,0:T(4,128)(2,1)} async-done(((bf16[8,1,4,6144]{3,2,1,0:T(4,128)(2,1)}), bf16[8,1,4,6144]{3,2,1,0:T(4,128)(2,1)}, u32[]{:S(2)}, u32[]{:S(2)}) %all-to-all-start.2) | async-done | bytes 393248 | tf_op jit(solution)/shard_map/all_to_all | solution.py:102
  514.6 1.8 reshape.95
  516.5 2.0 multiply_reduce_fusion
  518.5 0.6 fusion.22
  519.1 0.7 gather_fusion.1
  520.1 0.6 pad_maximum_fusion.1
  (38 shorter events, 1.6 us)
Async XLA Ops:
  7.2 323.0 %copy-start = (bf16[1,256,6144]{2,1,0:T(8,128)(2,1)S(1)}, bf16[1,256,6144]{2,1,0:T(8,128)(2,1)}, u32[]{:S(2)}) copy-start(bf16[1,256,6144]{2,1,0:T(8,128)(2,1)} %param.15) | copy-start | bytes 9437188
  7.2 487.7 %reduce-scatter.2.cloned.1.call-start = ((), (), s32[]{:S(2)}) async-start(), calls=%async_computation.4 | async-start | bytes 12976128 | tf_op jit(solution)/shard_map/reduce_scatter | solution.py:93
  36.3 289.5 %copy-start.5 = (bf16[1,6144,256]{2,1,0:T(8,128)(2,1)S(1)}, bf16[1,6144,256]{2,1,0:T(8,128)(2,1)}, u32[]{:S(2)}) copy-start(bf16[1,6144,256]{2,1,0:T(8,128)(2,1)} %param.13) | copy-start | bytes 9437188
  321.3 4.5 copy-start.2
  350.0 1.0 copy-start.3
  350.0 1.0 copy-start.4
  496.8 17.8 %all-to-all-start.2 = ((bf16[8,1,4,6144]{3,2,1,0:T(4,128)(2,1)}), bf16[8,1,4,6144]{3,2,1,0:T(4,128)(2,1)}, u32[]{:S(2)}, u32[]{:S(2)}) async-start(bf16[8,1,4,6144]{3,2,1,0:T(4,128)(2,1)} %bitcast.36), calls=%async_computation.3 | async-start | bytes 786432 | tf_op jit(solution)/shard_map/all_to_all | solution.py:102
  519.1 1.6 copy-start.1
Sparse Core Ops, SparseCore 0:
  350.2 144.6 reduce-scatter.1
